TPU v7x, 256 devices: a whole 4x4x8 slice. The times are simulated.
256 devices in a mesh: gx: 4 (over x), gy: 4 (over y), gz: 16 (over z, core).
Axes of the slice: x: 4, y: 4, z: 8, core: 2. Of those that a mesh axis runs over, the one named last changes fastest.
Arguments:
- densities: float32 [7, 512, 128, 512], P(None, 'gz', 'gy', 'gx'), may hold values from -6 to 6
- residuals: float32 [7, 512, 128, 512], P(None, 'gz', 'gy', 'gx'), may hold values from -320 to 320
Outputs:
- new_density: float32 [512, 128, 512], P('gz', 'gy', 'gx')
- weights: float32 [7], replicated
All inputs are finite; a program needn't handle non-finite values.
Results may differ from a plain program's by a relative error of at most 0.000087.
Values sent between devices are 32-bit elements; how exact they have to be, the bound alone decides.
A program may use at most 64 MiB of HBM per device.

v0:
```python
import math
import jax
import jax.numpy as jnp
from jax import lax
from jax.sharding import Mesh
from jax.sharding import PartitionSpec as P

SWEEPS = 3
GX_GY_GZ = ("gx", "gy", "gz_0", "gz_1")
GZ = ("gz_0", "gz_1")
shift_value = 0.15
mix_amount = 0.7


def extended(cells, sides, width):
    for axis, dim in sides:
        count = lax.axis_size(axis)
        head = lax.slice_in_dim(cells, 0, width, axis=dim)
        tail = lax.slice_in_dim(cells, cells.shape[dim] - width, cells.shape[dim], axis=dim)
        cells = jnp.concatenate(
            [
                lax.ppermute(tail, axis, [(i, (i + 1) % count) for i in range(count)]),
                cells,
                lax.ppermute(head, axis, [((i + 1) % count, i) for i in range(count)]),
            ],
            axis=dim,
        )
    return cells


def one_axis_at_a_time(shard, axes):
    for axis in axes:
        shard = lax.psum(shard, axis)
    return shard


def sweep_weights():
    diag_value = 6.0 + shift_value
    upper = (shift_value + 12.0) / diag_value
    lower = upper / 3.0
    return [
        1.0
        / (
            (upper + lower) / 2.0
            + (upper - lower) / 2.0 * math.cos(math.pi * (2 * k - 1) / (2 * SWEEPS))
        )
        for k in range(1, SWEEPS + 1)
    ]


def neighbours(padded):
    total = padded[:, 2:, 1:-1, 1:-1] + padded[:, :-2, 1:-1, 1:-1]
    total = total + padded[:, 1:-1, 2:, 1:-1] + padded[:, 1:-1, :-2, 1:-1]
    return total + padded[:, 1:-1, 1:-1, 2:] + padded[:, 1:-1, 1:-1, :-2]


def shrink(field):
    return field[:, 1:-1, 1:-1, 1:-1]


def relax(padded, rhs, omega):
    diag_value = 6.0 + shift_value
    centre = shrink(padded)
    return centre + omega * (rhs - diag_value * centre + neighbours(padded)) / diag_value


def precondition(fields):
    diag_value = 6.0 + shift_value
    omegas = sweep_weights()
    padded = extended(fields, (("gx", 3), ("gy", 2), (GZ, 1)), SWEEPS)
    rhs = 6.0 * shrink(padded) - neighbours(padded)
    iterate = omegas[0] * rhs / diag_value
    for position in range(1, SWEEPS):
        rhs = shrink(rhs)
        iterate = relax(iterate, rhs, omegas[position])
    return iterate


def on_device(densities, residuals):
    count = residuals.shape[0]
    flat = residuals.reshape(count, -1)
    local = jnp.dot(
        flat, flat.T, precision=lax.Precision.HIGHEST, preferred_element_type=jnp.float32
    )
    gram = one_axis_at_a_time(local, GX_GY_GZ)
    factor = jnp.linalg.cholesky(gram)
    ones_column = jnp.ones((count, 1), jnp.float32)
    middle = lax.linalg.triangular_solve(factor, ones_column, left_side=True, lower=True)
    solved = lax.linalg.triangular_solve(
        factor, middle, left_side=True, lower=True, transpose_a=True
    )[:, 0]
    weights = solved / jnp.sum(solved)
    blended = jnp.tensordot(weights, densities, axes=1, precision=lax.Precision.HIGHEST)
    combined = jnp.tensordot(weights, residuals, axes=1, precision=lax.Precision.HIGHEST)
    update = precondition(combined[None])[0]
    return (blended + mix_amount * update, weights)


def solution(mesh):
    torus = Mesh(
        mesh.devices.reshape(mesh.shape["gx"], mesh.shape["gy"], 8, 2), ("gx", "gy", "gz_0", "gz_1")
    )
    return jax.shard_map(
        on_device,
        mesh=torus,
        in_specs=(P(None, GZ, "gy", "gx"), P(None, GZ, "gy", "gx")),
        out_specs=(P(GZ, "gy", "gx"), P()),
        check_vma=False,
    )
```

profile of v0, /device:TPU:30, one launch (start us, length us, event | category | flops | bytes accessed | tf_op | source)
XLA Modules:
  0.0 109.0 jit_solution(10908965110666886729)
XLA Ops:
  0.6 14.5 %fusion.10 = f32[7,7]{0,1:T(8,128)S(1)} fusion(f32[7,32,32,128]{3,2,1,0:T(8,128)} %param.3), kind=kOutput, calls=%fused_computation.23 | convolution fusion | flops 77070336 | bytes 3670212 | tf_op jit(solution)/shard_map/dot_general | solution.py:82
  15.1 7.5 %psum.28 = f32[7,7]{0,1:T(8,128)S(1)} all-reduce(f32[7,7]{0,1:T(8,128)S(1)} %fusion.10), channel_id=1, replica_groups=mesh['gx'=4,'gy'=4,'gz_0'=8,'gz_1'=2] {'gx'}, use_global_device_ids=true, to_apply=%region_0.0 | all-reduce | flops 49 | bytes 392 | tf_op jit(solution)/shard_map/psum | solution.py:33
  22.6 8.0 %psum.29 = f32[7,7]{0,1:T(8,128)S(1)} all-reduce(f32[7,7]{0,1:T(8,128)S(1)} %psum.28), channel_id=1, replica_groups=mesh['gx'=4,'gy'=4,'gz_0'=8,'gz_1'=2] {'gy'}, use_global_device_ids=true, to_apply=%region_1.0 | all-reduce | flops 49 | bytes 392 | tf_op jit(solution)/shard_map/psum | solution.py:33
  30.5 19.5 %psum.30 = f32[7,7]{0,1:T(8,128)S(1)} all-reduce(f32[7,7]{0,1:T(8,128)S(1)} %psum.29), channel_id=1, replica_groups=mesh['gx'=4,'gy'=4,'gz_0'=8,'gz_1'=2] {'gz_0'}, use_global_device_ids=true, to_apply=%region_2.0 | all-reduce | flops 49 | bytes 392 | tf_op jit(solution)/shard_map/psum | solution.py:33
  50.0 2.5 %psum.31 = f32[7,7]{0,1:T(8,128)S(1)} all-reduce(f32[7,7]{0,1:T(8,128)S(1)} %psum.30), channel_id=1, replica_groups=mesh['gx'=4,'gy'=4,'gz_0'=8,'gz_1'=2] {'gz_1'}, use_global_device_ids=true, to_apply=%region_3.0 | all-reduce | flops 49 | bytes 392 | tf_op jit(solution)/shard_map/psum | solution.py:33
  52.6 0.6 cholesky.16
  53.2 0.6 compare_reduce_fusion
  53.9 0.6 fusion.19
  54.6 0.5 custom-call.8
  55.2 0.8 fusion.29
  56.0 0.6 broadcast_divide_fusion
  56.6 7.8 %fusion = f32[1,32,32,128]{3,0,2,1:T(1,128)S(1)} fusion(f32[7,32,32,128]{3,2,1,0:T(8,128)} %param.3, f32[7]{0:T(128)S(1)} %broadcast_divide_fusion), kind=kOutput, calls=%fused_computation | convolution fusion | flops 11010048 | bytes 4194332 | tf_op jit(solution)/shard_map/dot_general | solution.py:94
  64.7 3.6 %collective-permute-start = (f32[1,32,32,3]{3,2,1,0:T(8,128)S(1)}, f32[1,32,32,3]{3,2,1,0:T(8,128)S(1)}, u32[]{:S(2)}, u32[]{:S(2)}) collective-permute-start(f32[1,32,32,3]{3,2,1,0:T(8,128)S(1)} %get-tuple-element.8), channel_id=1, source_target_pairs={{0,64},{64,128},{128,192},{192,0},{1,65},{65,129},{129,193},{193,1... | collective-permute-start | bytes 36872 | tf_op jit(solution)/shard_map/ppermute | solution.py:22
  68.3 11.5 %collective-permute-done = f32[1,32,32,3]{3,2,1,0:T(8,128)S(1)} collective-permute-done((f32[1,32,32,3]{3,2,1,0:T(8,128)S(1)}, f32[1,32,32,3]{3,2,1,0:T(8,128)S(1)}, u32[]{:S(2)}, u32[]{:S(2)}) %collective-permute-start) | collective-permute-done | bytes 12320 | tf_op jit(solution)/shard_map/ppermute | solution.py:22
  79.8 3.4 %collective-permute-done.1 = f32[1,32,32,3]{3,2,1,0:T(8,128)S(1)} collective-permute-done((f32[1,32,32,3]{3,2,1,0:T(8,128)S(1)}, f32[1,32,32,3]{3,2,1,0:T(8,128)S(1)}, u32[]{:S(2)}, u32[]{:S(2)}) %collective-permute-start.1) | collective-permute-done | bytes 12320 | tf_op jit(solution)/shard_map/ppermute | solution.py:24
  83.5 3.6 %collective-permute-start.2 = (f32[1,32,3,134]{3,2,1,0:T(4,128)S(1)}, f32[1,32,3,134]{3,2,1,0:T(4,128)S(1)}, u32[]{:S(2)}, u32[]{:S(2)}) collective-permute-start(f32[1,32,3,134]{3,2,1,0:T(4,128)S(1)} %get-tuple-element.6), channel_id=1, source_target_pairs={{0,16},{16,32},{32,48},{48,0},{1,17},{17,33},{33,49},{49,1},{2,18}... | collective-permute-start | bytes 154376 | tf_op jit(solution)/shard_map/ppermute | solution.py:22
  87.1 2.5 %collective-permute-done.2 = f32[1,32,3,134]{3,2,1,0:T(4,128)S(1)} collective-permute-done((f32[1,32,3,134]{3,2,1,0:T(4,128)S(1)}, f32[1,32,3,134]{3,2,1,0:T(4,128)S(1)}, u32[]{:S(2)}, u32[]{:S(2)}) %collective-permute-start.2) | collective-permute-done | bytes 51488 | tf_op jit(solution)/shard_map/ppermute | solution.py:22
  89.6 3.7 %collective-permute-done.3 = f32[1,32,3,134]{3,2,1,0:T(4,128)S(1)} collective-permute-done((f32[1,32,3,134]{3,2,1,0:T(4,128)S(1)}, f32[1,32,3,134]{3,2,1,0:T(4,128)S(1)}, u32[]{:S(2)}, u32[]{:S(2)}) %collective-permute-start.3) | collective-permute-done | bytes 51488 | tf_op jit(solution)/shard_map/ppermute | solution.py:24
  93.5 2.9 %collective-permute-start.5 = (f32[1,3,38,134]{3,2,1,0:T(8,128)S(1)}, f32[1,3,38,134]{3,2,1,0:T(8,128)S(1)}, u32[]{:S(2)}, u32[]{:S(2)}) collective-permute-start(f32[1,3,38,134]{3,2,1,0:T(8,128)S(1)} %get-tuple-element.5), channel_id=1, source_target_pairs={{1,0},{2,1},{3,2},{4,3},{5,4},{6,5},{7,6},{8,7},{9,8},{10,9},{11,1... | collective-permute-start | bytes 183320 | tf_op jit(solution)/shard_map/ppermute | solution.py:24
  96.4 5.2 %fusion.4 = f32[1,32,32,128]{3,0,2,1:T(1,128)S(1)} fusion(f32[7,32,32,128]{3,2,1,0:T(8,128)S(1)} %copy-done, f32[7]{0:T(128)S(1)} %broadcast_divide_fusion), kind=kOutput, calls=%fused_computation.4 | convolution fusion | flops 11010048 | bytes 4194332 | tf_op jit(solution)/shard_map/dot_general | solution.py:93
  101.6 0.6 pad_maximum_fusion
  102.2 2.3 %broadcast_multiply_fusion = (f32[1,36,36,132]{3,2,1,0:T(8,128)S(1)}, f32[1,36,36,132]{3,2,1,0:T(8,128)S(1)}) fusion(f32[1,38,38,134]{3,2,1,0:T(8,128)S(1)} %pad_maximum_fusion), kind=kLoop, calls=%fused_computation.26 | loop fusion | flops 1368576 | bytes 6158592 | tf_op jit(solution)/shard_map/div | solution.py:72
  104.6 2.6 %fusion.9 = f32[1,34,34,130]{3,2,1,0:T(8,128)S(1)} fusion(f32[1,36,36,132]{3,2,1,0:T(8,128)S(1)} %get-tuple-element.2, f32[1,36,36,132]{3,2,1,0:T(8,128)S(1)} %get-tuple-element.3), kind=kLoop, calls=%fused_computation.17 | loop fusion | flops 1502800 | bytes 5410080 | tf_op jit(solution)/shard_map/add | solution.py:64
  107.2 1.8 %fusion.18 = f32[32,32,128]{2,1,0:T(8,128)} fusion(f32[32,32,128]{2,1,0:T(8,128)S(1)} %bitcast.45, f32[1,34,34,130]{3,2,1,0:T(8,128)S(1)} %fusion.9, f32[1,36,36,132]{3,2,1,0:T(8,128)S(1)} %get-tuple-element.3), kind=kLoop, calls=%fused_computation.33 | loop fusion | flops 1572864 | bytes 5242880 | tf_op jit(solution)/shard_map/add | solution.py:96
  (16 shorter events, 1.0 us)
Async XLA Ops:
  56.6 39.8 %copy-start.1 = (f32[7]{0:T(128)}, f32[7]{0:T(128)S(1)}, u32[]{:S(2)}) copy-start(f32[7]{0:T(128)S(1)} %broadcast_divide_fusion) | copy-start | bytes 88
  64.7 15.1 %collective-permute-start = (f32[1,32,32,3]{3,2,1,0:T(8,128)S(1)}, f32[1,32,32,3]{3,2,1,0:T(8,128)S(1)}, u32[]{:S(2)}, u32[]{:S(2)}) collective-permute-start(f32[1,32,32,3]{3,2,1,0:T(8,128)S(1)} %get-tuple-element.8), channel_id=1, source_target_pairs={{0,64},{64,128},{128,192},{192,0},{1,65},{65,129},{129,193},{193,1... | collective-permute-start | bytes 36872 | tf_op jit(solution)/shard_map/ppermute | solution.py:22
  68.3 14.9 %collective-permute-start.1 = (f32[1,32,32,3]{3,2,1,0:T(8,128)S(1)}, f32[1,32,32,3]{3,2,1,0:T(8,128)S(1)}, u32[]{:S(2)}, u32[]{:S(2)}) collective-permute-start(f32[1,32,32,3]{3,2,1,0:T(8,128)S(1)} %get-tuple-element.9), channel_id=1, source_target_pairs={{64,0},{128,64},{192,128},{0,192},{65,1},{129,65},{193,129},{1,193... | collective-permute-start | bytes 36872 | tf_op jit(solution)/shard_map/ppermute | solution.py:24
  83.2 13.2 %copy-start = (f32[7,32,32,128]{3,2,1,0:T(8,128)S(1)}, f32[7,32,32,128]{3,2,1,0:T(8,128)}, u32[]{:S(2)}) copy-start(f32[7,32,32,128]{3,2,1,0:T(8,128)} %param.2) | copy-start | bytes 11010052
  83.5 6.1 %collective-permute-start.2 = (f32[1,32,3,134]{3,2,1,0:T(4,128)S(1)}, f32[1,32,3,134]{3,2,1,0:T(4,128)S(1)}, u32[]{:S(2)}, u32[]{:S(2)}) collective-permute-start(f32[1,32,3,134]{3,2,1,0:T(4,128)S(1)} %get-tuple-element.6), channel_id=1, source_target_pairs={{0,16},{16,32},{32,48},{48,0},{1,17},{17,33},{33,49},{49,1},{2,18}... | collective-permute-start | bytes 154376 | tf_op jit(solution)/shard_map/ppermute | solution.py:22
  87.1 6.2 %collective-permute-start.3 = (f32[1,32,3,134]{3,2,1,0:T(4,128)S(1)}, f32[1,32,3,134]{3,2,1,0:T(4,128)S(1)}, u32[]{:S(2)}, u32[]{:S(2)}) collective-permute-start(f32[1,32,3,134]{3,2,1,0:T(4,128)S(1)} %get-tuple-element.7), channel_id=1, source_target_pairs={{16,0},{32,16},{48,32},{0,48},{17,1},{33,17},{49,33},{1,49},{18,2}... | collective-permute-start | bytes 154376 | tf_op jit(solution)/shard_map/ppermute | solution.py:24
  93.4 8.2 %collective-permute-start.4 = (f32[1,3,38,134]{3,2,1,0:T(8,128)S(1)}, f32[1,3,38,134]{3,2,1,0:T(8,128)S(1)}, u32[]{:S(2)}, u32[]{:S(2)}) collective-permute-start(f32[1,3,38,134]{3,2,1,0:T(8,128)S(1)} %get-tuple-element.4), channel_id=1, source_target_pairs={{0,1},{1,2},{2,3},{3,4},{4,5},{5,6},{6,7},{7,8},{8,9},{9,10},{10,1... | collective-permute-start | bytes 183320 | tf_op jit(solution)/shard_map/ppermute | solution.py:22
  93.5 8.1 %collective-permute-start.5 = (f32[1,3,38,134]{3,2,1,0:T(8,128)S(1)}, f32[1,3,38,134]{3,2,1,0:T(8,128)S(1)}, u32[]{:S(2)}, u32[]{:S(2)}) collective-permute-start(f32[1,3,38,134]{3,2,1,0:T(8,128)S(1)} %get-tuple-element.5), channel_id=1, source_target_pairs={{1,0},{2,1},{3,2},{4,3},{5,4},{6,5},{7,6},{8,7},{9,8},{10,9},{11,1... | collective-permute-start | bytes 183320 | tf_op jit(solution)/shard_map/ppermute | solution.py:24
where the time goes:
time: 109 us
  blocking collectives  37.4 us (34%)
  matrix products  28.4 us (26%)
  waiting for transfers between devices  21.1 us (19%)
  other arithmetic  11 us (10%)
  starting transfers between devices  10.1 us (9%)
    psum x4, blocking collectives, one_axis_at_a_time(): shard = lax.psum(shard, axis)  37.4 us
    dot_general x1, matrix products, on_device(): jnp.dot(flat, flat.T, precision=lax.Precision.HIGHEST, preferred_element_...  14.5 us
    ppermute x3, waiting for transfers between devices, extended(): lax.ppermute(tail, axis, [(i, (i + 1) % count) for i in range(count)])  14 us
    dot_general x1, matrix products, on_device(): jnp.tensordot(weights, residuals, axes=1, precision=lax.Precision.HIGHEST)  7.85 us
    ppermute x3, starting transfers between devices, extended(): lax.ppermute(tail, axis, [(i, (i + 1) % count) for i in range(count)])  7.18 us
    ppermute x3, waiting for transfers between devices, extended(): lax.ppermute(head, axis, [((i + 1) % count, i) for i in range(count)])  7.07 us
    dot_general x1, matrix products, on_device(): jnp.tensordot(weights, densities, axes=1, precision=lax.Precision.HIGHEST)  5.18 us
    ppermute x3, starting transfers between devices, extended(): lax.ppermute(head, axis, [((i + 1) % count, i) for i in range(count)])  2.95 us
  transfers between devices with their start and end apart: 6, of which 4 were waited for; matrix products, arithmetic and copies ran while one was open for 5% of the time, Pallas kernels for 0%

commit v1 on v0

--- a/solution.py
+++ b/solution.py
@@ -30,7 +30,7 @@
 
 def one_axis_at_a_time(shard, axes):
     for axis in axes:
-        shard = lax.psum(shard, axis)
+        shard = jnp.sum(lax.all_gather(shard, axis), axis=0)
     return shard
 
 

time: 109 us -> 122 us (1.12)
  blocking collectives: 37.4 us -> 54.3 us
  starting transfers between devices: 10.1 us -> 7.17 us
  waiting for transfers between devices: 21.1 us -> 18.6 us
    all_gather x0 -> x4, blocking collectives: none -> 54.3 us  [one_axis_at_a_time(): shard = jnp.sum(lax.all_gather(shard, axis), axis=0)]
    psum x4 -> x0, blocking collectives: 37.4 us -> none  [one_axis_at_a_time(): shard = lax.psum(shard, axis)]
    ppermute x3, starting transfers between devices: 7.18 us -> 1.77 us  [extended(): lax.ppermute(tail, axis, [(i, (i + 1) % count) for i in range(count)])]
    ppermute x3, waiting for transfers between devices: 7.07 us -> 3.74 us  [extended(): lax.ppermute(head, axis, [((i + 1) % count, i) for i in range(count)])]
    ppermute x3, starting transfers between devices: 2.95 us -> 5.4 us  [extended(): lax.ppermute(head, axis, [((i + 1) % count, i) for i in range(count)])]
  transfers between devices with their start and end apart: 6 -> 6, of which waited for: 4 -> 4; matrix products, arithmetic and copies ran while one was open for 5% -> 4% of each run, Pallas kernels for 0% -> 0%
where the time goes in v1:
time: 122 us
  blocking collectives  54.3 us (45%)
  matrix products  29.4 us (24%)
  waiting for transfers between devices  18.6 us (15%)
  other arithmetic  11 us (9%)
  starting transfers between devices  7.17 us (6%)
    all_gather x4, blocking collectives, one_axis_at_a_time(): shard = jnp.sum(lax.all_gather(shard, axis), axis=0)  54.3 us
    dot_general x1, matrix products, on_device(): jnp.dot(flat, flat.T, precision=lax.Precision.HIGHEST, preferred_element_...  15.5 us
    ppermute x3, waiting for transfers between devices, extended(): lax.ppermute(tail, axis, [(i, (i + 1) % count) for i in range(count)])  14.9 us
    dot_general x1, matrix products, on_device(): jnp.tensordot(weights, residuals, axes=1, precision=lax.Precision.HIGHEST)  7.85 us
    ppermute x3, starting transfers between devices, extended(): lax.ppermute(head, axis, [((i + 1) % count, i) for i in range(count)])  5.4 us
    dot_general x1, matrix products, on_device(): jnp.tensordot(weights, densities, axes=1, precision=lax.Precision.HIGHEST)  5.18 us
    ppermute x3, waiting for transfers between devices, extended(): lax.ppermute(head, axis, [((i + 1) % count, i) for i in range(count)])  3.74 us
    add x1, other arithmetic, relax(): centre + omega * (rhs - diag_value * centre + neighbours(padded)) / diag_...  2.59 us
  transfers between devices with their start and end apart: 6, of which 4 were waited for; matrix products, arithmetic and copies ran while one was open for 4% of the time, Pallas kernels for 0%

profile of v1, /device:TPU:30, one launch (start us, length us, event | category | flops | bytes accessed | tf_op | source)
XLA Modules:
  0.0 121.6 jit_solution(17874397126142215052)
XLA Ops:
  0.6 15.5 %fusion.10 = f32[1,7,7]{2,1,0:T(8,128)S(1)} fusion(f32[7,32,32,128]{3,2,1,0:T(8,128)} %param.3), kind=kOutput, calls=%fused_computation.23 | convolution fusion | flops 77070336 | bytes 3670212 | tf_op jit(solution)/shard_map/dot_general | solution.py:82
  16.1 12.0 %all-gather.4 = f32[4,7,7]{2,1,0:T(8,128)S(1)} all-gather(f32[1,7,7]{2,1,0:T(8,128)S(1)} %fusion.10), channel_id=2, replica_groups=mesh['gx'=4,'gy'=4,'gz_0'=8,'gz_1'=2] {'gx'}, dimensions={0}, use_global_device_ids=true | all-gather | bytes 980 | tf_op jit(solution)/shard_map/all_gather | solution.py:33
  28.1 12.0 %all-gather.5 = f32[4,7,7]{2,1,0:T(8,128)S(1)} all-gather(f32[1,7,7]{2,1,0:T(8,128)S(1)} %bitcast.54), channel_id=3, replica_groups=mesh['gx'=4,'gy'=4,'gz_0'=8,'gz_1'=2] {'gy'}, dimensions={0}, use_global_device_ids=true | all-gather | bytes 980 | tf_op jit(solution)/shard_map/all_gather | solution.py:33
  40.2 28.3 %all-gather.6 = f32[8,7,7]{2,1,0:T(8,128)S(1)} all-gather(f32[1,7,7]{2,1,0:T(8,128)S(1)} %bitcast.55), channel_id=4, replica_groups=mesh['gx'=4,'gy'=4,'gz_0'=8,'gz_1'=2] {'gz_0'}, dimensions={0}, use_global_device_ids=true | all-gather | bytes 1764 | tf_op jit(solution)/shard_map/all_gather | solution.py:33
  68.4 2.0 %all-gather.7 = f32[2,7,7]{2,1,0:T(8,128)S(1)} all-gather(f32[1,7,7]{2,1,0:T(8,128)S(1)} %bitcast.53), channel_id=5, replica_groups=mesh['gx'=4,'gy'=4,'gz_0'=8,'gz_1'=2] {'gz_1'}, dimensions={0}, use_global_device_ids=true | all-gather | bytes 588 | tf_op jit(solution)/shard_map/all_gather | solution.py:33
  71.2 0.6 compare_reduce_fusion
  71.9 0.6 fusion.19
  73.2 0.8 fusion.29
  73.9 0.6 broadcast_divide_fusion
  74.6 7.8 %fusion = f32[1,32,32,128]{3,0,2,1:T(1,128)S(1)} fusion(f32[7,32,32,128]{3,2,1,0:T(8,128)} %param.3, f32[7]{0:T(128)S(1)} %broadcast_divide_fusion), kind=kOutput, calls=%fused_computation | convolution fusion | flops 11010048 | bytes 4194332 | tf_op jit(solution)/shard_map/dot_general | solution.py:94
  82.7 0.9 collective-permute-start
  83.6 1.2 collective-permute-start.1
  84.8 12.0 %collective-permute-done = f32[1,32,32,3]{3,2,1,0:T(8,128)S(1)} collective-permute-done((f32[1,32,32,3]{3,2,1,0:T(8,128)S(1)}, f32[1,32,32,3]{3,2,1,0:T(8,128)S(1)}, u32[]{:S(2)}, u32[]{:S(2)}) %collective-permute-start) | collective-permute-done | bytes 12320 | tf_op jit(solution)/shard_map/ppermute | solution.py:22
  96.7 1.8 %collective-permute-done.1 = f32[1,32,32,3]{3,2,1,0:T(8,128)S(1)} collective-permute-done((f32[1,32,32,3]{3,2,1,0:T(8,128)S(1)}, f32[1,32,32,3]{3,2,1,0:T(8,128)S(1)}, u32[]{:S(2)}, u32[]{:S(2)}) %collective-permute-start.1) | collective-permute-done | bytes 12320 | tf_op jit(solution)/shard_map/ppermute | solution.py:24
  98.8 0.8 collective-permute-start.2
  99.6 1.3 %collective-permute-start.3 = (f32[1,32,3,134]{3,2,1,0:T(4,128)S(1)}, f32[1,32,3,134]{3,2,1,0:T(4,128)S(1)}, u32[]{:S(2)}, u32[]{:S(2)}) collective-permute-start(f32[1,32,3,134]{3,2,1,0:T(4,128)S(1)} %get-tuple-element.7), channel_id=1, source_target_pairs={{16,0},{32,16},{48,32},{0,48},{17,1},{33,17},{49,33},{1,49},{18,2}... | collective-permute-start | bytes 154376 | tf_op jit(solution)/shard_map/ppermute | solution.py:24
  100.9 2.9 %collective-permute-done.2 = f32[1,32,3,134]{3,2,1,0:T(4,128)S(1)} collective-permute-done((f32[1,32,3,134]{3,2,1,0:T(4,128)S(1)}, f32[1,32,3,134]{3,2,1,0:T(4,128)S(1)}, u32[]{:S(2)}, u32[]{:S(2)}) %collective-permute-start.2) | collective-permute-done | bytes 51488 | tf_op jit(solution)/shard_map/ppermute | solution.py:22
  103.8 2.0 %collective-permute-done.3 = f32[1,32,3,134]{3,2,1,0:T(4,128)S(1)} collective-permute-done((f32[1,32,3,134]{3,2,1,0:T(4,128)S(1)}, f32[1,32,3,134]{3,2,1,0:T(4,128)S(1)}, u32[]{:S(2)}, u32[]{:S(2)}) %collective-permute-start.3) | collective-permute-done | bytes 51488 | tf_op jit(solution)/shard_map/ppermute | solution.py:24
  106.0 2.9 %collective-permute-start.5 = (f32[1,3,38,134]{3,2,1,0:T(8,128)S(1)}, f32[1,3,38,134]{3,2,1,0:T(8,128)S(1)}, u32[]{:S(2)}, u32[]{:S(2)}) collective-permute-start(f32[1,3,38,134]{3,2,1,0:T(8,128)S(1)} %get-tuple-element.5), channel_id=1, source_target_pairs={{1,0},{2,1},{3,2},{4,3},{5,4},{6,5},{7,6},{8,7},{9,8},{10,9},{11,1... | collective-permute-start | bytes 183320 | tf_op jit(solution)/shard_map/ppermute | solution.py:24
  108.9 5.2 %fusion.4 = f32[1,32,32,128]{3,0,2,1:T(1,128)S(1)} fusion(f32[7,32,32,128]{3,2,1,0:T(8,128)S(1)} %copy-done, f32[7]{0:T(128)S(1)} %broadcast_divide_fusion), kind=kOutput, calls=%fused_computation.4 | convolution fusion | flops 11010048 | bytes 4194332 | tf_op jit(solution)/shard_map/dot_general | solution.py:93
  114.2 0.6 pad_maximum_fusion
  114.8 2.3 %broadcast_multiply_fusion = (f32[1,36,36,132]{3,2,1,0:T(8,128)S(1)}, f32[1,36,36,132]{3,2,1,0:T(8,128)S(1)}) fusion(f32[1,38,38,134]{3,2,1,0:T(8,128)S(1)} %pad_maximum_fusion), kind=kLoop, calls=%fused_computation.26 | loop fusion | flops 1368576 | bytes 6158592 | tf_op jit(solution)/shard_map/div | solution.py:72
  117.1 2.6 %fusion.9 = f32[1,34,34,130]{3,2,1,0:T(8,128)S(1)} fusion(f32[1,36,36,132]{3,2,1,0:T(8,128)S(1)} %get-tuple-element.2, f32[1,36,36,132]{3,2,1,0:T(8,128)S(1)} %get-tuple-element.3), kind=kLoop, calls=%fused_computation.17 | loop fusion | flops 1502800 | bytes 5410080 | tf_op jit(solution)/shard_map/add | solution.py:64
  119.7 1.8 %fusion.18 = f32[32,32,128]{2,1,0:T(8,128)} fusion(f32[32,32,128]{2,1,0:T(8,128)S(1)} %bitcast.52, f32[1,34,34,130]{3,2,1,0:T(8,128)S(1)} %fusion.9, f32[1,36,36,132]{3,2,1,0:T(8,128)S(1)} %get-tuple-element.3), kind=kLoop, calls=%fused_computation.33 | loop fusion | flops 1572864 | bytes 5242880 | tf_op jit(solution)/shard_map/add | solution.py:96
  (20 shorter events, 2.1 us)
Async XLA Ops:
  74.6 34.3 %copy-start.1 = (f32[7]{0:T(128)}, f32[7]{0:T(128)S(1)}, u32[]{:S(2)}) copy-start(f32[7]{0:T(128)S(1)} %broadcast_divide_fusion) | copy-start | bytes 88
  82.7 14.1 %collective-permute-start = (f32[1,32,32,3]{3,2,1,0:T(8,128)S(1)}, f32[1,32,32,3]{3,2,1,0:T(8,128)S(1)}, u32[]{:S(2)}, u32[]{:S(2)}) collective-permute-start(f32[1,32,32,3]{3,2,1,0:T(8,128)S(1)} %get-tuple-element.8), channel_id=1, source_target_pairs={{0,64},{64,128},{128,192},{192,0},{1,65},{65,129},{129,193},{193,1... | collective-permute-start | bytes 36872 | tf_op jit(solution)/shard_map/ppermute | solution.py:22
  83.6 14.9 %collective-permute-start.1 = (f32[1,32,32,3]{3,2,1,0:T(8,128)S(1)}, f32[1,32,32,3]{3,2,1,0:T(8,128)S(1)}, u32[]{:S(2)}, u32[]{:S(2)}) collective-permute-start(f32[1,32,32,3]{3,2,1,0:T(8,128)S(1)} %get-tuple-element.9), channel_id=1, source_target_pairs={{64,0},{128,64},{192,128},{0,192},{65,1},{129,65},{193,129},{1,193... | collective-permute-start | bytes 36872 | tf_op jit(solution)/shard_map/ppermute | solution.py:24
  98.5 10.4 %copy-start = (f32[7,32,32,128]{3,2,1,0:T(8,128)S(1)}, f32[7,32,32,128]{3,2,1,0:T(8,128)}, u32[]{:S(2)}) copy-start(f32[7,32,32,128]{3,2,1,0:T(8,128)} %param.2) | copy-start | bytes 11010052
  98.8 5.0 %collective-permute-start.2 = (f32[1,32,3,134]{3,2,1,0:T(4,128)S(1)}, f32[1,32,3,134]{3,2,1,0:T(4,128)S(1)}, u32[]{:S(2)}, u32[]{:S(2)}) collective-permute-start(f32[1,32,3,134]{3,2,1,0:T(4,128)S(1)} %get-tuple-element.6), channel_id=1, source_target_pairs={{0,16},{16,32},{32,48},{48,0},{1,17},{17,33},{33,49},{49,1},{2,18}... | collective-permute-start | bytes 154376 | tf_op jit(solution)/shard_map/ppermute | solution.py:22
  99.6 6.2 %collective-permute-start.3 = (f32[1,32,3,134]{3,2,1,0:T(4,128)S(1)}, f32[1,32,3,134]{3,2,1,0:T(4,128)S(1)}, u32[]{:S(2)}, u32[]{:S(2)}) collective-permute-start(f32[1,32,3,134]{3,2,1,0:T(4,128)S(1)} %get-tuple-element.7), channel_id=1, source_target_pairs={{16,0},{32,16},{48,32},{0,48},{17,1},{33,17},{49,33},{1,49},{18,2}... | collective-permute-start | bytes 154376 | tf_op jit(solution)/shard_map/ppermute | solution.py:24
  106.0 8.2 %collective-permute-start.4 = (f32[1,3,38,134]{3,2,1,0:T(8,128)S(1)}, f32[1,3,38,134]{3,2,1,0:T(8,128)S(1)}, u32[]{:S(2)}, u32[]{:S(2)}) collective-permute-start(f32[1,3,38,134]{3,2,1,0:T(8,128)S(1)} %get-tuple-element.4), channel_id=1, source_target_pairs={{0,1},{1,2},{2,3},{3,4},{4,5},{5,6},{6,7},{7,8},{8,9},{9,10},{10,1... | collective-permute-start | bytes 183320 | tf_op jit(solution)/shard_map/ppermute | solution.py:22
  106.0 8.1 %collective-permute-start.5 = (f32[1,3,38,134]{3,2,1,0:T(8,128)S(1)}, f32[1,3,38,134]{3,2,1,0:T(8,128)S(1)}, u32[]{:S(2)}, u32[]{:S(2)}) collective-permute-start(f32[1,3,38,134]{3,2,1,0:T(8,128)S(1)} %get-tuple-element.5), channel_id=1, source_target_pairs={{1,0},{2,1},{3,2},{4,3},{5,4},{6,5},{7,6},{8,7},{9,8},{10,9},{11,1... | collective-permute-start | bytes 183320 | tf_op jit(solution)/shard_map/ppermute | solution.py:24
